TPU v7x, 32 devices: a whole 2x2x4 slice. The times are simulated.
32 devices in a mesh: owner: 4 (over y, core), rows: 8 (over z, x).
Axes of the slice: x: 2, y: 2, z: 4, core: 2. Of those that a mesh axis runs over, the one named last changes fastest.
Arguments:
- train_gate: float32 [64, 2048, 1024], P('owner', 'rows'), may hold values from -0.1875 to 0.1875
- other_gate: bfloat16 [64, 2048, 1024], P('owner', 'rows'), may hold values from -0.0625 to 0.0625
- train_up: float32 [64, 2048, 1024], P('owner', 'rows'), may hold values from -0.1875 to 0.1875
- other_up: bfloat16 [64, 2048, 1024], P('owner', 'rows'), may hold values from -0.0625 to 0.0625
- train_down: float32 [64, 1024, 2048], P('owner', None, 'rows'), may hold values from -0.25 to 0.25
- other_down: bfloat16 [64, 1024, 2048], P('owner', None, 'rows'), may hold values from -0.09375 to 0.09375
- router_weight: float32 [2048, 64], P('rows', 'owner'), may hold values from -0.125 to 0.125
- router_gain: float32 [2048], P('rows'), may hold values from 0.25 to 1.75
Outputs:
- ready_gate: bfloat16 [64, 2048, 1024], P('owner', None, 'rows')
- ready_up: bfloat16 [64, 2048, 1024], P('owner', None, 'rows')
- ready_down: bfloat16 [64, 1024, 2048], P('owner', 'rows')
- scale_gate: float32 [64, 1024], P('owner', 'rows')
- scale_up: float32 [64, 1024], P('owner', 'rows')
- scale_down: float32 [64, 1024], P('owner', 'rows')
- serve_router: bfloat16 [2048, 64], replicated
All inputs are finite; a program needn't handle non-finite values. Where the computation divides by a largest or mean magnitude, that divisor is 1e-20 or more.
Results may differ from a plain program's by a relative error of at most 0.001.
Values may be sent and summed in bfloat16 or wider, within the bound.
A program may use at most 192 MiB of HBM per device.

v0:
```python
import jax
import jax.numpy as jnp
from jax import lax
from jax.sharding import PartitionSpec as P


def shards(
    train_gate, other_gate, train_up, other_up, train_down, other_down, router_weight, router_gain
):
    latest_gate = train_gate + other_gate.astype(jnp.float32)
    latest_up = train_up + other_up.astype(jnp.float32)
    latest_down = train_down + other_down.astype(jnp.float32)
    scale_gate, scale_up, scale_down = lax.pmax(
        (
            jnp.max(jnp.abs(latest_gate), axis=1),
            jnp.max(jnp.abs(latest_up), axis=1),
            jnp.max(jnp.abs(latest_down), axis=2),
        ),
        "rows",
    )
    narrow_gate, narrow_up, narrow_down = (
        (latest_gate / jnp.expand_dims(scale_gate, 1)).astype(jnp.bfloat16),
        (latest_up / jnp.expand_dims(scale_up, 1)).astype(jnp.bfloat16),
        (latest_down / jnp.expand_dims(scale_down, 2)).astype(jnp.bfloat16),
    )
    ready_gate, ready_up = (
        lax.all_to_all(narrow_gate, "rows", split_axis=2, concat_axis=1, tiled=True),
        lax.all_to_all(narrow_up, "rows", split_axis=2, concat_axis=1, tiled=True),
    )
    ready_down = lax.all_to_all(narrow_down, "rows", split_axis=1, concat_axis=2, tiled=True)
    scale_gate = lax.dynamic_slice_in_dim(
        scale_gate, lax.axis_index("rows") * ready_gate.shape[2], ready_gate.shape[2], axis=1
    )
    scale_up = lax.dynamic_slice_in_dim(
        scale_up, lax.axis_index("rows") * ready_up.shape[2], ready_up.shape[2], axis=1
    )
    scale_down = lax.dynamic_slice_in_dim(
        scale_down, lax.axis_index("rows") * ready_down.shape[1], ready_down.shape[1], axis=1
    )
    part_router = (router_weight * router_gain[:, None]).astype(jnp.bfloat16)
    row_router = lax.all_gather(part_router, "rows", axis=0, tiled=True)
    serve_router = lax.all_gather(row_router, "owner", axis=1, tiled=True)
    return (ready_gate, ready_up, ready_down, scale_gate, scale_up, scale_down, serve_router)


def solution(mesh):
    placed = (
        P("owner", "rows", None),
        P("owner", "rows", None),
        P("owner", "rows", None),
        P("owner", "rows", None),
        P("owner", None, "rows"),
        P("owner", None, "rows"),
        P("rows", "owner"),
        P("rows"),
    )
    return jax.shard_map(
        shards,
        mesh=mesh,
        in_specs=placed,
        out_specs=(
            P("owner", None, "rows"),
            P("owner", None, "rows"),
            P("owner", "rows", None),
            P("owner", "rows"),
            P("owner", "rows"),
            P("owner", "rows"),
            P(),
        ),
        check_vma=False,
    )
```

profile of v0, /device:TPU:0, one launch (start us, length us, event | category | flops | bytes accessed | tf_op | source)
XLA Modules:
  0.0 877.2 jit_solution(6322543164802641597)
XLA Ops:
  7.2 0.0 all-reduce.3.cloned.1.call-start
  7.2 17.6 %copy.34 = f32[16,256,1024]{1,0,2:T(8,128)} copy(f32[16,256,1024]{2,1,0:T(8,128)} %param.10) | data formatting | bytes 33554432 | tf_op args[2]
  24.8 12.5 %copy.33 = bf16[16,256,1024]{1,0,2:T(8,128)(2,1)} copy(bf16[16,256,1024]{2,1,0:T(8,128)(2,1)} %param.11) | data formatting | bytes 16777216 | tf_op args[3]
  37.3 17.6 %copy.31 = f32[16,256,1024]{1,0,2:T(8,128)} copy(f32[16,256,1024]{2,1,0:T(8,128)} %param.8) | data formatting | bytes 33554432 | tf_op args[0]
  54.9 12.5 %copy.30 = bf16[16,256,1024]{1,0,2:T(8,128)(2,1)} copy(bf16[16,256,1024]{2,1,0:T(8,128)(2,1)} %param.9) | data formatting | bytes 16777216 | tf_op args[1]
  67.4 11.1 %abs_reduce_fusion.1 = f32[16,1024]{0,1:T(8,128)} fusion(f32[16,256,1024]{1,0,2:T(8,128)} %copy.34, bf16[16,256,1024]{1,0,2:T(8,128)(2,1)} %copy.33), kind=kLoop, calls=%fused_computation.4 | loop fusion | flops 16760832 | bytes 25231360 | tf_op jit(solution)/shard_map/reduce_max | solution.py:16
  78.5 2.1 copy-done
  80.6 2.4 copy-done.1
  83.0 4.3 abs_reduce_fusion.2
  87.3 0.0 slice-done
  87.3 29.3 %abs_reduce_fusion = f32[16,1024]{0,1:T(8,128)} fusion(f32[16,1024,256]{2,1,0:T(8,128)} %param.12, bf16[16,1024,256]{2,1,0:T(8,128)(2,1)S(1)} %bitcast.14), kind=kLoop, calls=%fused_computation.2 | loop fusion | flops 16760832 | bytes 25231360 | tf_op jit(solution)/shard_map/reduce_max | solution.py:17
  116.5 0.0 all-reduce.3.cloned.1.call-update
  116.6 92.5 %all-reduce.3.cloned.1.call-done = (f32[16,1024]{0,1:T(8,128)}, f32[16,1024]{0,1:T(8,128)}, f32[16,1024]{0,1:T(8,128)}) async-done(((f32[16,1024]{0,1:T(8,128)}, f32[16,1024]{0,1:T(8,128)}, f32[16,1024]{0,1:T(8,128)}), (f32[16,1024]{0,1:T(8,128)}, f32[16,1024]{0,1:T(8,128)}, f32[16,1024]{0,1:T(8,128)})) %all-reduce.3.cloned.1.call-update) | async-done | bytes 196624 | tf_op jit(solution)/shard_map/pmax | solution.py:13
  209.0 20.5 %divide_convert_fusion.1 = (bf16[16,256,1024]{1,0,2:T(8,128)(2,1)}, bf16[16,256,1024]{1,0,2:T(8,128)(2,1)S(1)}) fusion(f32[16,256,1024]{1,0,2:T(8,128)} %copy.34, bf16[16,256,1024]{1,0,2:T(8,128)(2,1)} %copy.33, f32[16,1024]{0,1:T(8,128)} %get-tuple-element.15, f32[16,1024]{0,1:T(8,128)} %get-tuple-element.14, f32[16,256,1024]{1,0,2:T(8,128)} %copy.31, ...), kind=kLoop, calls=%fused_computation.3 | loop fusion | flops 33554432 | bytes 67239936 | tf_op jit(solution)/shard_map/convert_element_type | solution.py:23
  229.6 187.0 %all_to_all.54 = bf16[16,256,1024]{1,0,2:T(8,128)(2,1)} all-to-all(bf16[16,256,1024]{1,0,2:T(8,128)(2,1)S(1)} %get-tuple-element.18), channel_id=1, replica_groups=mesh['owner'=4,'rows'=8] {'rows'}, dimensions={2} | all-to-all | bytes 16777216 | tf_op jit(solution)/shard_map/all_to_all | solution.py:27
  416.6 4.9 all-to-all-start.1
  421.5 23.8 %divide_convert_fusion = bf16[16,1024,256]{2,0,1:T(8,128)(2,1)} fusion(f32[16,1024,256]{2,1,0:T(8,128)} %param.12, f32[16,1024]{0,1:T(8,128)S(1)} %copy-done.2, bf16[16,1024,256]{2,1,0:T(8,128)(2,1)} %param.13), kind=kLoop, calls=%fused_computation.1 | loop fusion | flops 16777216 | bytes 33619968 | tf_op jit(solution)/shard_map/convert_element_type | solution.py:24
  445.3 158.3 %all-to-all-done.1 = bf16[16,256,1024]{1,0,2:T(8,128)(2,1)} async-done(((bf16[16,256,1024]{1,0,2:T(8,128)(2,1)}), bf16[16,256,1024]{1,0,2:T(8,128)(2,1)}, u32[]{:S(2)}, u32[]{:S(2)}) %all-to-all-start.1) | async-done | bytes 8388640 | tf_op jit(solution)/shard_map/all_to_all | solution.py:28
  603.6 5.0 all-to-all-start.2
  608.7 201.9 %all_gather.6 = bf16[2048,16]{0,1:T(8,128)(2,1)S(1)} all-gather(bf16[256,16]{0,1:T(8,128)(2,1)S(1)} %multiply_convert_fusion), channel_id=1, replica_groups=mesh['owner'=4,'rows'=8] {'rows'}, dimensions={0}, use_global_device_ids=true | all-gather | bytes 73728 | tf_op jit(solution)/shard_map/all_gather | solution.py:41
  810.6 6.0 all_gather.7
  816.5 0.8 constant_dynamic-slice_fusion
  817.4 0.7 copy.40
  818.1 0.7 copy.41
  818.7 0.8 constant_dynamic-slice_fusion.2
  819.6 0.7 copy.39
  820.2 12.3 %copy.32 = bf16[16,8,256,128]{3,2,1,0:T(8,128)(2,1)} copy(bf16[16,8,256,128]{2,0,3,1:T(8,128)(2,1)} %bitcast.15) | data formatting | bytes 16777216 | tf_op jit(solution)/shard_map/all_to_all | solution.py:27
  832.5 12.3 %copy.35 = bf16[16,8,256,128]{3,2,1,0:T(8,128)(2,1)} copy(bf16[16,8,256,128]{2,0,3,1:T(8,128)(2,1)} %bitcast.4) | data formatting | bytes 16777216 | tf_op jit(solution)/shard_map/all_to_all | solution.py:28
  844.8 0.0 all-to-all-done.2
  844.8 11.4 %copy.38 = bf16[16,128,8,256]{3,2,1,0:T(8,128)(2,1)} copy(bf16[16,128,8,256]{3,0,1,2:T(8,128)(2,1)} %bitcast.7) | data formatting | bytes 16777216 | tf_op jit(solution)/shard_map/all_to_all | solution.py:30
  856.2 13.4 %all_to_all.50 = bf16[16,128,2048]{2,1,0:T(8,128)(2,1)} reshape(bf16[16,128,8,256]{3,2,1,0:T(8,128)(2,1)} %copy.38) | data formatting | bytes 16777216 | tf_op jit(solution)/shard_map/all_to_all | solution.py:30
  869.6 0.7 copy.53
  (13 shorter events, 0.0 us)
Async XLA Ops:
  7.2 201.9 %all-reduce.3.cloned.1.call-start = ((), (), s32[]{:S(2)}) async-start(), calls=%async_computation.3 | async-start | bytes 3145728 | tf_op jit(solution)/shard_map/pmax | solution.py:13
  67.4 13.2 %copy-start = (f32[16,256,1024]{1,0,2:T(8,128)S(1)}, f32[16,256,1024]{1,0,2:T(8,128)}, u32[]{:S(2)}) copy-start(f32[16,256,1024]{1,0,2:T(8,128)} %copy.31) | copy-start | bytes 50331652
  67.4 15.6 %copy-start.1 = (bf16[16,256,1024]{1,0,2:T(8,128)(2,1)S(1)}, bf16[16,256,1024]{1,0,2:T(8,128)(2,1)}, u32[]{:S(2)}) copy-start(bf16[16,256,1024]{1,0,2:T(8,128)(2,1)} %copy.30) | copy-start | bytes 25165828
  67.4 19.9 %slice-start = ((s8[8388608]{0:T(1024)(128)(4,1)}), s8[4194304]{0:T(1024)(128)(4,1)S(1)}, s32[]{:S(2)}) async-start(s8[8388608]{0:T(1024)(128)(4,1)} %bitcast.13), calls=%async_computation.4 | async-start | bytes 8388608
  83.0 4.3 slice-start.1
  229.6 192.0 %copy-start.2 = (f32[16,1024]{0,1:T(8,128)S(1)}, f32[16,1024]{0,1:T(8,128)}, u32[]{:S(2)}) copy-start(f32[16,1024]{0,1:T(8,128)} %get-tuple-element.16) | copy-start | bytes 196612
  416.6 187.0 %all-to-all-start.1 = ((bf16[16,256,1024]{1,0,2:T(8,128)(2,1)}), bf16[16,256,1024]{1,0,2:T(8,128)(2,1)}, u32[]{:S(2)}, u32[]{:S(2)}) async-start(bf16[16,256,1024]{1,0,2:T(8,128)(2,1)} %get-tuple-element.17), calls=%async_computation.1 | async-start | bytes 16777216 | tf_op jit(solution)/shard_map/all_to_all | solution.py:28
  445.3 163.3 %copy-start.3 = (f32[256,16]{0,1:T(8,128)S(1)}, f32[256,16]{0,1:T(8,128)}, u32[]{:S(2)}) copy-start(f32[256,16]{0,1:T(8,128)} %param.14) | copy-start | bytes 49156
  445.3 163.3 %copy-start.4 = (f32[256]{0:T(256)S(1)}, f32[256]{0:T(256)}, u32[]{:S(2)}) copy-start(f32[256]{0:T(256)} %param.15) | copy-start | bytes 3076
  603.6 241.2 %all-to-all-start.2 = ((bf16[16,1024,256]{2,0,1:T(8,128)(2,1)}), bf16[16,1024,256]{2,0,1:T(8,128)(2,1)}, u32[]{:S(2)}, u32[]{:S(2)}) async-start(bf16[16,1024,256]{2,0,1:T(8,128)(2,1)} %divide_convert_fusion), calls=%async_computation.2 | async-start | bytes 16777216 | tf_op jit(solution)/shard_map/all_to_all | solution.py:30
Sparse Core Ops, SparseCore 0:
  116.7 92.2 all-reduce.2
where the time goes:
time: 880 us; the launch traced here: 877 us
  blocking collectives  395 us (45%)
  waiting for transfers between devices  251 us (29%)
  local copies, waits for them, and re-layouts  118 us (13%)
  other arithmetic  88.9 us (10%)
  between operations  14.1 us (2%)
  starting transfers between devices  10 us (1%)
    all_gather x1, blocking collectives, shards(): row_router = lax.all_gather(part_router, 'rows', axis=0, tiled=True)  202 us
    all_to_all x1, blocking collectives, shards(): lax.all_to_all(narrow_gate, 'rows', split_axis=2, concat_axis=1, tiled=True)  187 us
    all_to_all x1, waiting for transfers between devices, shards(): lax.all_to_all(narrow_up, 'rows', split_axis=2, concat_axis=1, tiled=True)  158 us
    pmax x1, waiting for transfers between devices, shards(): lax.pmax((jnp.max(jnp.abs(latest_gate), axis=1), jnp.max(jnp.abs(latest_u...  92.5 us
    unnamed x22, local copies, waits for them, and re-layouts  67.4 us
    reduce_max x1, other arithmetic, shards(): jnp.max(jnp.abs(latest_down), axis=2)  29.3 us
    all_to_all x2, local copies, waits for them, and re-layouts, shards(): lax.all_to_all(narrow_down, 'rows', split_axis=1, concat_axis=2, tiled=True)  24.8 us
    convert_element_type x1, other arithmetic, shards(): (latest_down / jnp.expand_dims(scale_down, 2)).astype(jnp.bfloat16)  23.8 us
  transfers between devices with their start and end apart: 3, of which 2 were waited for; matrix products, arithmetic and copies ran while one was open for 6% of the time, Pallas kernels for 0%

commit v1 on v0

--- a/solution.py
+++ b/solution.py
@@ -1,7 +1,19 @@
+import functools
 import jax
 import jax.numpy as jnp
 from jax import lax
 from jax.sharding import PartitionSpec as P
+
+
+def _process_members_all(x_in, axis_id):
+    x_now = jnp.concatenate(
+        lax.all_to_all(jnp.stack(jnp.split(x_in, lax.axis_size(axis_id), axis=2)), axis_id, 0, 0),
+        axis=1,
+    )
+    return x_now
+
+
+lay_works = functools.partial(_process_members_all, axis_id="rows")
 
 
 def shards(
@@ -25,7 +37,7 @@
     )
     ready_gate, ready_up = (
         lax.all_to_all(narrow_gate, "rows", split_axis=2, concat_axis=1, tiled=True),
-        lax.all_to_all(narrow_up, "rows", split_axis=2, concat_axis=1, tiled=True),
+        lay_works(narrow_up),
     )
     ready_down = lax.all_to_all(narrow_down, "rows", split_axis=1, concat_axis=2, tiled=True)
     scale_gate = lax.dynamic_slice_in_dim(

time: 880 us -> 822 us (0.934)
  blocking collectives: 395 us -> 208 us
  waiting for transfers between devices: 251 us -> 404 us
  local copies, waits for them, and re-layouts: 118 us -> 88.5 us
    all_to_all x1 -> x0, blocking collectives: 187 us -> none  [shards(): lax.all_to_all(narrow_gate, 'rows', split_axis=2, concat_axis=1, tiled=True)]
    all_to_all x1 -> x2, waiting for transfers between devices: 158 us -> 321 us  [the longest x1 163 us: shards(): lax.all_to_all(narrow_gate, 'rows', split_axis=2, concat_axis=1, tiled=True)]
    unnamed x22 -> x28, local copies, waits for them, and re-layouts: 67.4 us -> 40.9 us
    all_to_all x1 -> x0, local copies, waits for them, and re-layouts: 12.3 us -> none  [shards(): lax.all_to_all(narrow_up, 'rows', split_axis=2, concat_axis=1, tiled=True)]
    convert_element_type x0 -> x1, other arithmetic: none -> 12.1 us  [shards(): (latest_gate / jnp.expand_dims(scale_gate, 1)).astype(jnp.bfloat16)]
    convert_element_type x1, other arithmetic: 20.5 us -> 9.39 us  [shards(): (latest_up / jnp.expand_dims(scale_up, 1)).astype(jnp.bfloat16)]
    pmax x1, waiting for transfers between devices: 92.5 us -> 82.4 us  [shards(): lax.pmax((jnp.max(jnp.abs(latest_gate), axis=1), jnp.max(jnp.abs(latest_u...]
  transfers between devices with their start and end apart: 3 -> 4, of which waited for: 2 -> 3; matrix products, arithmetic and copies ran while one was open for 6% -> 8% of each run, Pallas kernels for 0% -> 0%
where the time goes in v1:
time: 822 us; the launch traced here: 820 us
  waiting for transfers between devices  404 us (49%)
  blocking collectives  208 us (25%)
  other arithmetic  90.5 us (11%)
  local copies, waits for them, and re-layouts  88.5 us (11%)
  starting transfers between devices  15.3 us (2%)
  between operations  14.1 us (2%)
    all_gather x1, blocking collectives, shards(): row_router = lax.all_gather(part_router, 'rows', axis=0, tiled=True)  202 us
    all_to_all x1, waiting for transfers between devices, shards(): lax.all_to_all(narrow_gate, 'rows', split_axis=2, concat_axis=1, tiled=True)  163 us
    all_to_all x1, waiting for transfers between devices, _process_members_all(): lax.all_to_all(jnp.stack(jnp.split(x_in, lax.axis_size(axis_id), axis=2))...  158 us
    pmax x1, waiting for transfers between devices, shards(): lax.pmax((jnp.max(jnp.abs(latest_gate), axis=1), jnp.max(jnp.abs(latest_u...  82.4 us
    unnamed x28, local copies, waits for them, and re-layouts  40.9 us
    all_to_all x2, local copies, waits for them, and re-layouts, shards(): lax.all_to_all(narrow_down, 'rows', split_axis=1, concat_axis=2, tiled=True)  24.8 us
    reduce_max x1, other arithmetic, shards(): jnp.max(jnp.abs(latest_down), axis=2)  24.4 us
    convert_element_type x1, other arithmetic, shards(): (latest_down / jnp.expand_dims(scale_down, 2)).astype(jnp.bfloat16)  23.8 us
  transfers between devices with their start and end apart: 4, of which 3 were waited for; matrix products, arithmetic and copies ran while one was open for 8% of the time, Pallas kernels for 0%

profile of v1, /device:TPU:0, one launch (start us, length us, event | category | flops | bytes accessed | tf_op | source)
XLA Modules:
  0.0 820.4 jit_solution(3453497732132076611)
XLA Ops:
  7.2 17.6 %copy.28 = f32[16,256,1024]{1,0,2:T(8,128)} copy(f32[16,256,1024]{2,1,0:T(8,128)} %param.8) | data formatting | bytes 33554432 | tf_op args[0]
  24.8 12.5 %copy.27 = bf16[16,256,1024]{1,0,2:T(8,128)(2,1)} copy(bf16[16,256,1024]{2,1,0:T(8,128)(2,1)} %param.9) | data formatting | bytes 16777216 | tf_op args[1]
  37.3 11.1 %abs_reduce_fusion.2 = f32[16,1024]{0,1:T(8,128)} fusion(f32[16,256,1024]{1,0,2:T(8,128)} %copy.28, bf16[16,256,1024]{1,0,2:T(8,128)(2,1)} %copy.27), kind=kLoop, calls=%fused_computation.7 | loop fusion | flops 16760832 | bytes 25231360 | tf_op jit(solution)/shard_map/reduce_max | solution.py:27
  48.4 9.8 %abs_reduce_fusion.1 = f32[16,1024]{1,0:T(8,128)} fusion(f32[16,256,1024]{2,1,0:T(8,128)} %param.10, bf16[16,256,1024]{2,1,0:T(8,128)(2,1)} %param.11), kind=kLoop, calls=%fused_computation.4 | loop fusion | flops 16760832 | bytes 25231360 | tf_op jit(solution)/shard_map/reduce_max | solution.py:28
  58.2 24.4 %abs_reduce_fusion = f32[16,1024]{0,1:T(8,128)} fusion(f32[16,1024,256]{2,1,0:T(8,128)S(1)} %bitcast.44, bf16[16,1024,256]{2,1,0:T(8,128)(2,1)} %param.13), kind=kLoop, calls=%fused_computation.2 | loop fusion | flops 16760832 | bytes 25231360 | tf_op jit(solution)/shard_map/reduce_max | solution.py:29
  82.6 82.4 %all-reduce.3.cloned.1.call-done = (f32[16,1024]{0,1:T(8,128)}, f32[16,1024]{1,0:T(8,128)}, f32[16,1024]{0,1:T(8,128)}) async-done(((f32[16,1024]{0,1:T(8,128)}, f32[16,1024]{1,0:T(8,128)}, f32[16,1024]{0,1:T(8,128)}), (f32[16,1024]{0,1:T(8,128)}, f32[16,1024]{1,0:T(8,128)}, f32[16,1024]{0,1:T(8,128)})) %all-reduce.3.cloned.1.call-update) | async-done | bytes 196624 | tf_op jit(solution)/shard_map/pmax | solution.py:25
  165.0 12.1 %divide_convert_fusion.2 = bf16[16,256,1024]{1,0,2:T(8,128)(2,1)} fusion(f32[16,256,1024]{1,0,2:T(8,128)} %copy.28, bf16[16,256,1024]{1,0,2:T(8,128)(2,1)} %copy.27, f32[16,1024]{0,1:T(8,128)} %get-tuple-element.14), kind=kLoop, calls=%fused_computation.6 | loop fusion | flops 16777216 | bytes 33619968 | tf_op jit(solution)/shard_map/convert_element_type | solution.py:34
  177.1 5.3 all-to-all-start
  182.3 9.4 %divide_convert_fusion.1 = bf16[16,256,1024]{2,1,0:T(8,128)(2,1)S(1)} fusion(f32[16,256,1024]{2,1,0:T(8,128)} %param.10, bf16[16,256,1024]{2,1,0:T(8,128)(2,1)} %param.11, f32[16,1024]{1,0:T(8,128)S(1)} %copy-done.1), kind=kLoop, calls=%fused_computation.3 | loop fusion | flops 16777216 | bytes 33619968 | tf_op jit(solution)/shard_map/convert_element_type | solution.py:35
  191.7 1.2 fusion.7
  193.0 1.2 fusion.6
  194.2 1.2 fusion.5
  195.5 1.2 fusion.4
  196.7 1.2 fusion.3
  198.0 1.2 fusion.2
  199.2 1.2 fusion.1
  200.5 1.2 fusion
  201.7 163.3 %all-to-all-done = bf16[16,256,1024]{1,0,2:T(8,128)(2,1)} async-done(((bf16[16,256,1024]{1,0,2:T(8,128)(2,1)}), bf16[16,256,1024]{1,0,2:T(8,128)(2,1)}, u32[]{:S(2)}, u32[]{:S(2)}) %all-to-all-start) | async-done | bytes 8388640 | tf_op jit(solution)/shard_map/all_to_all | solution.py:39
  365.0 5.0 all-to-all-start.1
  370.0 23.8 %divide_convert_fusion = bf16[16,1024,256]{2,0,1:T(8,128)(2,1)} fusion(f32[16,1024,256]{2,1,0:T(8,128)} %param.12, f32[16,1024]{0,1:T(8,128)S(1)} %copy-done, bf16[16,1024,256]{2,1,0:T(8,128)(2,1)} %param.13), kind=kLoop, calls=%fused_computation.1 | loop fusion | flops 16777216 | bytes 33619968 | tf_op jit(solution)/shard_map/convert_element_type | solution.py:36
  393.8 158.2 %all-to-all-done.1 = bf16[8,16,256,128]{3,2,1,0:T(8,128)(2,1)} async-done(((bf16[8,16,256,128]{3,2,1,0:T(8,128)(2,1)}), bf16[8,16,256,128]{3,2,1,0:T(8,128)(2,1)}, u32[]{:S(2)}, u32[]{:S(2)}) %all-to-all-start.1) | async-done | bytes 8388640 | tf_op jit(solution)/shard_map/all_to_all | solution.py:10
  552.0 5.0 all-to-all-start.2
  557.0 202.1 %all_gather.6 = bf16[2048,16]{0,1:T(8,128)(2,1)S(1)} all-gather(bf16[256,16]{0,1:T(8,128)(2,1)S(1)} %multiply_convert_fusion), channel_id=1, replica_groups=mesh['owner'=4,'rows'=8] {'rows'}, dimensions={0}, use_global_device_ids=true | all-gather | bytes 73728 | tf_op jit(solution)/shard_map/all_gather | solution.py:53
  759.1 6.0 all_gather.7
  765.1 0.8 constant_dynamic-slice_fusion
  766.0 0.7 copy.34
  766.6 0.7 copy.35
  767.9 12.3 %copy.29 = bf16[16,8,256,128]{3,2,1,0:T(8,128)(2,1)} copy(bf16[16,8,256,128]{2,0,3,1:T(8,128)(2,1)} %bitcast.1) | data formatting | bytes 16777216 | tf_op jit(solution)/shard_map/all_to_all | solution.py:39
  780.2 7.9 copy.30
  788.1 11.4 %copy.33 = bf16[16,128,8,256]{3,2,1,0:T(8,128)(2,1)} copy(bf16[16,128,8,256]{3,0,1,2:T(8,128)(2,1)} %bitcast.14) | data formatting | bytes 16777216 | tf_op jit(solution)/shard_map/all_to_all | solution.py:42
  799.4 13.4 %all_to_all.37 = bf16[16,128,2048]{2,1,0:T(8,128)(2,1)} reshape(bf16[16,128,8,256]{3,2,1,0:T(8,128)(2,1)} %copy.33) | data formatting | bytes 16777216 | tf_op jit(solution)/shard_map/all_to_all | solution.py:42
  812.9 0.7 copy.54
  (22 shorter events, 0.7 us)
Async XLA Ops:
  7.2 157.8 %all-reduce.3.cloned.1.call-start = ((), (), s32[]{:S(2)}) async-start(), calls=%async_computation.3 | async-start | bytes 2228224 | tf_op jit(solution)/shard_map/pmax | solution.py:25
  37.3 20.9 %slice-start = ((s8[16777216]{0:T(1024)(128)(4,1)}), s8[4194304]{0:T(1024)(128)(4,1)S(1)}, s32[]{:S(2)}) async-start(s8[16777216]{0:T(1024)(128)(4,1)} %bitcast.43), calls=%async_computation.4 | async-start | bytes 8388608
  37.3 20.9 %slice-start.1 = ((s8[16777216]{0:T(1024)(128)(4,1)}), s8[4194304]{0:T(1024)(128)(4,1)S(1)}, s32[]{:S(2)}) async-start(s8[16777216]{0:T(1024)(128)(4,1)} %bitcast.43), calls=%async_computation.5 | async-start | bytes 8388608
  37.3 20.9 %slice-start.2 = ((s8[16777216]{0:T(1024)(128)(4,1)}), s8[4194304]{0:T(1024)(128)(4,1)S(1)}, s32[]{:S(2)}) async-start(s8[16777216]{0:T(1024)(128)(4,1)} %bitcast.43), calls=%async_computation.6 | async-start | bytes 8388608
  48.4 9.8 %slice-start.3 = ((s8[16777216]{0:T(1024)(128)(4,1)}), s8[4194304]{0:T(1024)(128)(4,1)S(1)}, s32[]{:S(2)}) async-start(s8[16777216]{0:T(1024)(128)(4,1)} %bitcast.43), calls=%async_computation.7 | async-start | bytes 8388608
  177.1 5.3 copy-start.1
  177.1 187.9 %all-to-all-start = ((bf16[16,256,1024]{1,0,2:T(8,128)(2,1)}), bf16[16,256,1024]{1,0,2:T(8,128)(2,1)}, u32[]{:S(2)}, u32[]{:S(2)}) async-start(bf16[16,256,1024]{1,0,2:T(8,128)(2,1)} %divide_convert_fusion.2), calls=%async_computation | async-start | bytes 16777216 | tf_op jit(solution)/shard_map/all_to_all | solution.py:39
  201.7 168.3 %copy-start = (f32[16,1024]{0,1:T(8,128)S(1)}, f32[16,1024]{0,1:T(8,128)}, u32[]{:S(2)}) copy-start(f32[16,1024]{0,1:T(8,128)} %get-tuple-element.16) | copy-start | bytes 196612
  365.0 187.1 %all-to-all-start.1 = ((bf16[8,16,256,128]{3,2,1,0:T(8,128)(2,1)}), bf16[8,16,256,128]{3,2,1,0:T(8,128)(2,1)}, u32[]{:S(2)}, u32[]{:S(2)}) async-start(bf16[8,16,256,128]{3,2,1,0:T(8,128)(2,1)} %fusion), calls=%async_computation.1 | async-start | bytes 16777216 | tf_op jit(solution)/shard_map/all_to_all | solution.py:10
  393.8 163.2 %copy-start.2 = (f32[256,16]{0,1:T(8,128)S(1)}, f32[256,16]{0,1:T(8,128)}, u32[]{:S(2)}) copy-start(f32[256,16]{0,1:T(8,128)} %param.14) | copy-start | bytes 49156
  393.8 163.2 %copy-start.3 = (f32[256]{0:T(256)S(1)}, f32[256]{0:T(256)}, u32[]{:S(2)}) copy-start(f32[256]{0:T(256)} %param.15) | copy-start | bytes 3076
  552.0 236.0 %all-to-all-start.2 = ((bf16[16,1024,256]{2,0,1:T(8,128)(2,1)}), bf16[16,1024,256]{2,0,1:T(8,128)(2,1)}, u32[]{:S(2)}, u32[]{:S(2)}) async-start(bf16[16,1024,256]{2,0,1:T(8,128)(2,1)} %divide_convert_fusion), calls=%async_computation.2 | async-start | bytes 16777216 | tf_op jit(solution)/shard_map/all_to_all | solution.py:42
Sparse Core Ops, SparseCore 0:
  82.7 82.2 all-reduce.2
